TPU v7x, 128 devices: a whole 4x4x4 slice. The times are simulated.
128 devices in a mesh: pipe: 2 (over x_lo), tensor: 4 (over x_hi, core), dp: 16 (over z, y).
Axes of the slice: x: 4 (x_hi: 2, x_lo: 2; x = x_hi * 2 + x_lo), y: 4, z: 4, core: 2. Of those that a mesh axis runs over, the one named last changes fastest.
Arguments:
- inputs: bfloat16 [2, 2048, 16384], P(None, 'dp', 'tensor'), may hold values from -6 to 6
- w_in: bfloat16 [2, 16384, 1024], P('pipe', ('tensor', 'dp')), may hold values from -0.046875 to 0.046875
- w_out: bfloat16 [2, 1024, 16384], P('pipe', None, ('tensor', 'dp')), may hold values from -0.1875 to 0.1875
- cotangent: bfloat16 [2, 2048, 16384], P(None, 'dp', 'tensor'), may hold values from -6 to 6
Outputs:
- update_in: float32 [2, 16384, 1024], P('pipe', ('tensor', 'dp'))
- update_out: float32 [2, 1024, 16384], P('pipe', None, ('tensor', 'dp'))
- grad_norm: float32 [], replicated
All inputs are finite; a program needn't handle non-finite values.
Results may differ from a plain program's by a relative error of at most 0.008.
Values may be sent and summed in bfloat16 or wider, within the bound.
A program may use at most 192 MiB of HBM per device.

v0:
```python
import jax
import jax.numpy as jnp
from jax import lax
from jax.sharding import Mesh
from jax.sharding import PartitionSpec as P

CLIP_NORM = 16384
DP = ("dp_0", "dp_1")
TENSOR = ("tensor_0", "tensor_1")
PIPE_TENSOR_DP = ("pipe", "tensor_0", "tensor_1", "dp_0", "dp_1")
TENSOR_DP = ("tensor_0", "tensor_1", "dp_0", "dp_1")


def rows_first(arrays, axis, dims):
    turned = [jnp.moveaxis(a, dim, 0) for a, dim in zip(arrays, dims)]
    both = jnp.concatenate([t.reshape(len(t), -1) for t in turned], axis=1)
    filled, at, done = (lax.all_gather(both, axis, axis=0, tiled=True), 0, [])
    for t, dim in zip(turned, dims):
        section = filled[:, at : at + t[0].size].reshape(-1, *t.shape[1:])
        done.append(jnp.moveaxis(section, 0, dim))
        at += t[0].size
    return tuple(done)


def total_of_pieces(value, axis):
    return lax.all_gather(value, axis).sum(0)


def from_behind(value, axis, by):
    count = lax.axis_size(axis)
    pairs = [(i, i + by) for i in range(count) if 0 <= i + by < count]
    return lax.ppermute(value, axis, pairs)


def by_axis(value, axes):
    for axis in axes:
        value = lax.psum(value, axis)
    return value


def unit_forward(preact, unused):
    return jax.nn.silu(preact).astype(jnp.bfloat16)


def unit_backward(upward, preact):
    sigmoid_value = jax.nn.sigmoid(preact)
    return (upward * sigmoid_value * (1.0 + preact * (1.0 - sigmoid_value))).astype(jnp.bfloat16)


def kahan_add(running, carried, grad_term):
    corrected = grad_term - carried.astype(jnp.float32)
    summed = (running.astype(jnp.float32) + corrected).astype(jnp.bfloat16)
    carried = (summed.astype(jnp.float32) - running.astype(jnp.float32) - corrected).astype(
        jnp.bfloat16
    )
    return (summed, carried)


def contract_last(first_operand, second_operand):
    return lax.dot_general(
        first_operand, second_operand, (((1,), (1,)), ((), ())), preferred_element_type=jnp.float32
    )


def keep_state(state, x_part, act_part, err_part, slope_part):
    return state


def on_device(inputs, w_in, w_out, cotangent):
    sections = lax.axis_size("pipe")
    section_index = lax.axis_index("pipe")
    micro_count = inputs.shape[0]
    step_count = micro_count + sections - 1
    w_first, w_second = rows_first((w_in[0], w_out[0]), DP, (0, 1))
    section_inputs, section_seeds = (inputs, cotangent)
    groups = 1
    stat_rows = section_inputs.shape[1]

    def combine_units(partial_value, unit_fn, kept_stat):
        whole_sum = total_of_pieces(partial_value, TENSOR)
        return (whole_sum, unit_fn(whole_sum, kept_stat))

    row_count = section_inputs.shape[1]
    col_count = section_inputs.shape[2]
    hidden = w_first.shape[1]
    zero_stat = jnp.zeros((stat_rows, hidden), jnp.float32)
    zero_rows = jnp.zeros((row_count, col_count), jnp.bfloat16)
    zero_units = jnp.zeros((row_count, hidden), jnp.float32)

    def project_in(current):
        return jnp.dot(current, w_first, preferred_element_type=jnp.float32)

    def project_back(current):
        return contract_last(current, w_second)

    def no_units(current):
        return zero_units

    def residual_forward(current, activation):
        return (
            current.astype(jnp.float32)
            + jnp.dot(activation, w_second, preferred_element_type=jnp.float32)
        ).astype(jnp.bfloat16)

    def residual_backward(current, slope):
        return (current.astype(jnp.float32) + contract_last(slope, w_first)).astype(jnp.bfloat16)

    def no_rows(current, other):
        return zero_rows

    def forward_step(state_carry, step_index):
        incoming, kept_x, kept_pre, kept_act = state_carry
        micro_index = step_index - section_index
        active = jnp.logical_and(micro_index >= 0, micro_index < micro_count)
        micro_slot = jnp.clip(micro_index, 0, micro_count - 1)
        own_rows = lax.dynamic_index_in_dim(section_inputs, micro_slot, 0, False)
        current = jnp.where(section_index == 0, own_rows, incoming)
        partial_value = lax.cond(active, project_in, no_units, current)
        preact, activation = combine_units(partial_value, unit_forward, zero_stat)
        result = lax.cond(active, residual_forward, no_rows, current, activation)
        kept_x = jnp.where(
            active, lax.dynamic_update_index_in_dim(kept_x, current, micro_slot, 0), kept_x
        )
        kept_pre = jnp.where(
            active, lax.dynamic_update_index_in_dim(kept_pre, preact, micro_slot, 0), kept_pre
        )
        kept_act = jnp.where(
            active, lax.dynamic_update_index_in_dim(kept_act, activation, micro_slot, 0), kept_act
        )
        outgoing = from_behind(result, "pipe", 1)
        return ((outgoing, kept_x, kept_pre, kept_act), None)

    forward_init = (
        zero_rows,
        jnp.zeros((micro_count, row_count, col_count), jnp.bfloat16),
        jnp.zeros((micro_count, stat_rows, hidden), jnp.float32),
        jnp.zeros((micro_count, row_count, hidden), jnp.bfloat16),
    )
    forward_final, unused_out = lax.scan(forward_step, forward_init, jnp.arange(step_count))
    unused_rows, kept_x, kept_pre, kept_act = forward_final

    def accumulate(state, x_part, act_part, err_part, slope_part):
        sum_in, err_in, sum_out, err_out = state
        x_groups = x_part.reshape(groups, -1, col_count)
        slope_groups = slope_part.reshape(groups, -1, hidden)
        act_groups = act_part.reshape(groups, -1, hidden)
        err_groups = err_part.reshape(groups, -1, col_count)
        grad_in = jnp.einsum(
            "gtc,gth->gch", x_groups, slope_groups, preferred_element_type=jnp.float32
        )
        grad_out = jnp.einsum(
            "gth,gtc->ghc", act_groups, err_groups, preferred_element_type=jnp.float32
        )
        sum_in, err_in = kahan_add(sum_in, err_in, grad_in)
        sum_out, err_out = kahan_add(sum_out, err_out, grad_out)
        return (sum_in, err_in, sum_out, err_out)

    def backward_step(state_carry, step_index):
        incoming, sums = state_carry
        micro_index = step_index - (sections - 1 - section_index)
        active = jnp.logical_and(micro_index >= 0, micro_index < micro_count)
        micro_slot = jnp.clip(micro_index, 0, micro_count - 1)
        own_rows = lax.dynamic_index_in_dim(section_seeds, micro_slot, 0, False)
        current = jnp.where(section_index == sections - 1, own_rows, incoming)
        partial_value = lax.cond(active, project_back, no_units, current)
        preact = lax.dynamic_index_in_dim(kept_pre, micro_slot, 0, False)
        unused_stat, slope = combine_units(partial_value, unit_backward, preact)
        x_here = lax.dynamic_index_in_dim(kept_x, micro_slot, 0, False)
        act_here = lax.dynamic_index_in_dim(kept_act, micro_slot, 0, False)
        sums = lax.cond(active, accumulate, keep_state, sums, x_here, act_here, current, slope)
        result = lax.cond(active, residual_backward, no_rows, current, slope)
        outgoing = from_behind(result, "pipe", -1)
        return ((outgoing, sums), None)

    sums_init = (
        jnp.zeros((groups, col_count, hidden), jnp.bfloat16),
        jnp.zeros((groups, col_count, hidden), jnp.bfloat16),
        jnp.zeros((groups, hidden, col_count), jnp.bfloat16),
        jnp.zeros((groups, hidden, col_count), jnp.bfloat16),
    )
    backward_final, unused_back = lax.scan(
        backward_step, (zero_rows, sums_init), jnp.arange(step_count)
    )
    unused_errors, final_sums = backward_final
    sum_in, err_in, sum_out, err_out = final_sums
    total_in = jnp.sum(sum_in.astype(jnp.float32) - err_in.astype(jnp.float32), axis=0)
    total_out = jnp.sum(sum_out.astype(jnp.float32) - err_out.astype(jnp.float32), axis=0)
    total_in, total_out = (
        lax.psum_scatter(total_in, DP, scatter_dimension=0, tiled=True),
        lax.psum_scatter(total_out, DP, scatter_dimension=1, tiled=True),
    )
    squares = jnp.sum(total_in * total_in) + jnp.sum(total_out * total_out)
    norm_squared = by_axis(squares, PIPE_TENSOR_DP)
    grad_norm = jnp.sqrt(norm_squared)
    factor = jnp.minimum(1.0, CLIP_NORM / grad_norm)
    return ((total_in * factor)[None], (total_out * factor)[None], grad_norm)


def solution(mesh):
    split = Mesh(
        mesh.devices.reshape(mesh.shape["pipe"], 2, 2, 4, 4),
        ("pipe", "tensor_0", "tensor_1", "dp_0", "dp_1"),
    )
    placed = (
        P(None, DP, TENSOR),
        P("pipe", TENSOR_DP, None),
        P("pipe", None, TENSOR_DP),
        P(None, DP, TENSOR),
    )
    return jax.shard_map(
        on_device,
        mesh=split,
        in_specs=placed,
        out_specs=(P("pipe", TENSOR_DP, None), P("pipe", None, TENSOR_DP), P()),
        check_vma=False,
    )
```

profile of v0, /device:TPU:0, one launch (start us, length us, event | category | flops | bytes accessed | tf_op | source)
XLA Modules:
  0.0 888.3 jit_solution(17027753523874269229)
XLA Ops:
  10.6 114.0 %all-gather.10.cloned.1.call-done = bf16[4096,2048]{1,0:T(8,128)(2,1)} async-done(((bf16[256,2048]{1,0:T(8,128)(2,1)}), bf16[4096,2048]{1,0:T(8,128)(2,1)}) %all-gather.10.cloned.1.call-update) | async-done | bytes 16777232 | tf_op jit(solution)/shard_map/all_gather | solution.py:17
  124.6 11.7 %fusion.32 = (bf16[4096,1024]{1,0:T(8,128)(2,1)}, bf16[1024,4096]{0,1:T(8,128)(2,1)}) fusion(bf16[4096,2048]{1,0:T(8,128)(2,1)} %all-gather.10.cloned.1.call-done), kind=kLoop, calls=%fused_computation.55 | loop fusion | bytes 33554432 | tf_op jit(solution)/shard_map/slice | solution.py:19
  136.3 11.3 %copy.9 = bf16[1024,4096]{1,0:T(8,128)(2,1)} copy(bf16[1024,4096]{0,1:T(8,128)(2,1)} %get-tuple-element.500) | data formatting | bytes 16777216 | tf_op jit(solution)/shard_map/while | solution.py:181
  150.4 213.6 %while.37 = (s32[]{:T(128)}, bf16[128,4096]{1,0:T(8,128)(2,1)}, bf16[2,128,4096]{2,1,0:T(8,128)(2,1)}, f32[2,128,1024]{2,1,0:T(8,128)S(1)}, bf16[2,128,1024]{2,1...) while((s32[]{:T(128)}, bf16[128,4096]{1,0:T(8,128)(2,1)}, ...), condition=%wide.region_6.7_spmd, body=%wide.region_0.6_spmd.sunk | while | flops 2152071168 | bytes 50332584 | solution.py:139
  160.3 26.3 %all-gather.12.cloned.1.call-done = f32[512,1024]{1,0:T(8,128)} async-done(((f32[128,1024]{1,0:T(8,128)}), f32[512,1024]{1,0:T(8,128)}) %all-gather.12.cloned.1.call-update) | async-done | bytes 2097168 | tf_op jit(solution)/shard_map/while/body/eval_jaxpr/all_gather | solution.py:26
  195.9 23.0 %collective-permute-done = bf16[128,4096]{1,0:T(8,128)(2,1)S(1)} collective-permute-done((bf16[128,4096]{1,0:T(8,128)(2,1)}, bf16[128,4096]{1,0:T(8,128)(2,1)S(1)}, u32[]{:S(2)}, u32[]{:S(2)}) %collective-permute-start) | collective-permute-done | bytes 1048608 | tf_op jit(solution)/shard_map/while/body/eval_jaxpr/ppermute | solution.py:32
  229.8 27.7 %all-gather.12.cloned.1.call-done = f32[512,1024]{1,0:T(8,128)} async-done(((f32[128,1024]{1,0:T(8,128)}), f32[512,1024]{1,0:T(8,128)}) %all-gather.12.cloned.1.call-update) | async-done | bytes 2097168 | tf_op jit(solution)/shard_map/while/body/eval_jaxpr/all_gather | solution.py:26
  267.9 22.8 %collective-permute-done = bf16[128,4096]{1,0:T(8,128)(2,1)S(1)} collective-permute-done((bf16[128,4096]{1,0:T(8,128)(2,1)}, bf16[128,4096]{1,0:T(8,128)(2,1)S(1)}, u32[]{:S(2)}, u32[]{:S(2)}) %collective-permute-start) | collective-permute-done | bytes 1048608 | tf_op jit(solution)/shard_map/while/body/eval_jaxpr/ppermute | solution.py:32
  297.0 32.9 %all-gather.12.cloned.1.call-done = f32[512,1024]{1,0:T(8,128)} async-done(((f32[128,1024]{1,0:T(8,128)}), f32[512,1024]{1,0:T(8,128)}) %all-gather.12.cloned.1.call-update) | async-done | bytes 2097168 | tf_op jit(solution)/shard_map/while/body/eval_jaxpr/all_gather | solution.py:26
  340.3 22.8 %collective-permute-done = bf16[128,4096]{1,0:T(8,128)(2,1)S(1)} collective-permute-done((bf16[128,4096]{1,0:T(8,128)(2,1)}, bf16[128,4096]{1,0:T(8,128)(2,1)S(1)}, u32[]{:S(2)}, u32[]{:S(2)}) %collective-permute-start) | collective-permute-done | bytes 1048608 | tf_op jit(solution)/shard_map/while/body/eval_jaxpr/ppermute | solution.py:32
  381.7 218.9 %while.38 = (s32[]{:T(128)}, bf16[128,4096]{1,0:T(8,128)(2,1)S(1)}, bf16[1,4096,1024]{2,1,0:T(8,128)(2,1)}, bf16[1,4096,1024]{2,1,0:T(8,128)(2,1)}, bf16[1,1024,...) while((s32[]{:T(128)}, bf16[128,4096]{1,0:T(8,128)(2,1)S(1)}, ...), condition=%wide.region_15.16_spmd, body=%wide.region_7.15_spmd.sunk | while | flops 4374134784 | bytes 187172016 | solution.py:181
  385.4 34.3 %all-gather.14.cloned.1.call-done = f32[512,1024]{1,0:T(8,128)} async-done(((f32[128,1024]{1,0:T(8,128)}), f32[512,1024]{1,0:T(8,128)}) %all-gather.14.cloned.1.call-update) | async-done | bytes 2097168 | tf_op jit(solution)/shard_map/while/body/eval_jaxpr/all_gather | solution.py:26
  424.1 30.4 %collective-permute-done.1 = bf16[128,4096]{1,0:T(8,128)(2,1)S(1)} collective-permute-done((bf16[128,4096]{1,0:T(8,128)(2,1)}, bf16[128,4096]{1,0:T(8,128)(2,1)S(1)}, u32[]{:S(2)}, u32[]{:S(2)}) %collective-permute-start.1) | collective-permute-done | bytes 1048608 | tf_op jit(solution)/shard_map/while/body/eval_jaxpr/ppermute | solution.py:32
  464.3 27.5 %all-gather.14.cloned.1.call-done = f32[512,1024]{1,0:T(8,128)} async-done(((f32[128,1024]{1,0:T(8,128)}), f32[512,1024]{1,0:T(8,128)}) %all-gather.14.cloned.1.call-update) | async-done | bytes 2097168 | tf_op jit(solution)/shard_map/while/body/eval_jaxpr/all_gather | solution.py:26
  502.4 25.6 %conditional.14 = ((bf16[1,4096,1024]{2,1,0:T(8,128)(2,1)}, bf16[1,4096,1024]{2,1,0:T(8,128)(2,1)}, bf16[1,1024,4096]{2,1,0:T(8,128)(2,1)}, bf16[1,1024,4096]{2,1,0:T(8,128)(2,1)})) conditional(s32[]{:T(128)} %convert_element_type.173, (bf16[1,4096,1024]{2,1,0:T(8,128)(2,1)}, bf16[1,4096,1024]{2,1,0:T(8,128)(2,1)}, ...), branch_computations={%region_13.13_spmd, %region_14.14_spmd} | conditional | flops 2222981120 | bytes 136839776 | solution.py:170
  502.5 12.9 %fusion.12 = (bf16[1,4096,1024]{2,1,0:T(8,128)(2,1)}, bf16[1,4096,1024]{2,1,0:T(8,128)(2,1)}) fusion(bf16[1,4096,1024]{2,1,0:T(8,128)(2,1)} %get-tuple-element.369, bf16[1,4096,1024]{2,1,0:T(8,128)(2,1)} %get-tuple-element.373, bf16[128,1024]{1,0:T(8,128)(2,1)S(1)} %get-tuple-element.372, bf16[2,128,4096]{2,1,0:T(8,128)(2,1)} %get-tuple-element.370, ...), kind=kOutput, calls=%fused_computation.24 | convolution fusion | flops 1111490560 | bytes 34865664 | tf_op jit(solution)/shard_map/while/body/eval_jaxpr/cond/branch_1_fun/gtc,gth->gch/dot_general | solution.py:148
  538.3 25.6 %all-gather.14.cloned.1.call-done = f32[512,1024]{1,0:T(8,128)} async-done(((f32[128,1024]{1,0:T(8,128)}), f32[512,1024]{1,0:T(8,128)}) %all-gather.14.cloned.1.call-update) | async-done | bytes 2097168 | tf_op jit(solution)/shard_map/while/body/eval_jaxpr/all_gather | solution.py:26
  574.5 25.6 %conditional.14 = ((bf16[1,4096,1024]{2,1,0:T(8,128)(2,1)}, bf16[1,4096,1024]{2,1,0:T(8,128)(2,1)}, bf16[1,1024,4096]{2,1,0:T(8,128)(2,1)}, bf16[1,1024,4096]{2,1,0:T(8,128)(2,1)})) conditional(s32[]{:T(128)} %convert_element_type.173, (bf16[1,4096,1024]{2,1,0:T(8,128)(2,1)}, bf16[1,4096,1024]{2,1,0:T(8,128)(2,1)}, ...), branch_computations={%region_13.13_spmd, %region_14.14_spmd} | conditional | flops 2222981120 | bytes 136839776 | solution.py:170
  574.5 12.9 %fusion.12 = (bf16[1,4096,1024]{2,1,0:T(8,128)(2,1)}, bf16[1,4096,1024]{2,1,0:T(8,128)(2,1)}) fusion(bf16[1,4096,1024]{2,1,0:T(8,128)(2,1)} %get-tuple-element.369, bf16[1,4096,1024]{2,1,0:T(8,128)(2,1)} %get-tuple-element.373, bf16[128,1024]{1,0:T(8,128)(2,1)S(1)} %get-tuple-element.372, bf16[2,128,4096]{2,1,0:T(8,128)(2,1)} %get-tuple-element.370, ...), kind=kOutput, calls=%fused_computation.24 | convolution fusion | flops 1111490560 | bytes 34865664 | tf_op jit(solution)/shard_map/while/body/eval_jaxpr/cond/branch_1_fun/gtc,gth->gch/dot_general | solution.py:148
  600.6 12.2 %subtract_bitcast_fusion = f32[1024,4096]{1,0:T(8,128)} fusion(bf16[1,1024,4096]{2,1,0:T(8,128)(2,1)} %get-tuple-element.414, bf16[1,1024,4096]{2,1,0:T(8,128)(2,1)} %get-tuple-element.413), kind=kLoop, calls=%fused_computation.47 | loop fusion | flops 12582912 | bytes 33554432 | tf_op jit(solution)/shard_map/reduce_sum | solution.py:187
  612.8 13.3 %subtract_bitcast_fusion.1 = f32[4096,1024]{1,0:T(8,128)} fusion(bf16[1,4096,1024]{2,1,0:T(8,128)(2,1)} %get-tuple-element.412, bf16[1,4096,1024]{2,1,0:T(8,128)(2,1)} %get-tuple-element.411), kind=kLoop, calls=%fused_computation.48 | loop fusion | flops 12582912 | bytes 33554432 | tf_op jit(solution)/shard_map/reduce_sum | solution.py:186
  626.1 96.8 %reduce-scatter.5.cloned.1.call-done = f32[1024,256]{1,0:T(8,128)} async-done(((f32[1024,4096]{1,0:T(8,128)}), f32[1024,256]{1,0:T(8,128)}) %reduce-scatter.5.cloned.1.call-update) | async-done | bytes 1048592 | tf_op jit(solution)/shard_map/reduce_scatter | solution.py:190
  725.0 111.5 %reduce-scatter.3.cloned.1.call-done = f32[256,1024]{1,0:T(8,128)} async-done(((f32[4096,1024]{1,0:T(8,128)}), f32[256,1024]{1,0:T(8,128)}) %reduce-scatter.3.cloned.1.call-update) | async-done | bytes 1048592 | tf_op jit(solution)/shard_map/reduce_scatter | solution.py:189
  855.4 10.5 %psum.38 = f32[]{:T(128)} all-reduce(f32[]{:T(128)} %psum.37), channel_id=1, replica_groups=mesh['pipe'=2,'tensor_0'=2,'tensor_1'=2,'dp_0'=4,'dp_1'=4] {'dp_0'}, use_global_device_ids=true, to_apply=%region_23.24 | all-reduce | flops 1 | bytes 8 | tf_op jit(solution)/shard_map/psum | solution.py:37
  (144 shorter events, 233.4 us)
Async XLA Ops:
  7.2 117.4 %all-gather.10.cloned.1.call-start = ((), (), s32[]{:S(2)}) async-start(), calls=%async_computation.2 | async-start | bytes 17825792 | tf_op jit(solution)/shard_map/all_gather | solution.py:17
  150.4 36.2 %all-gather.12.cloned.1.call-start = ((), (), s32[]{:S(2)}) async-start(), calls=%async_computation.5 | async-start | bytes 2621440 | tf_op jit(solution)/shard_map/while/body/eval_jaxpr/all_gather | solution.py:26
  194.3 24.7 %collective-permute-start = (bf16[128,4096]{1,0:T(8,128)(2,1)}, bf16[128,4096]{1,0:T(8,128)(2,1)S(1)}, u32[]{:S(2)}, u32[]{:S(2)}) collective-permute-start(bf16[128,4096]{1,0:T(8,128)(2,1)} %get-tuple-element.782), channel_id=1, source_target_pairs={{0,64},{1,65},{2,66},{3,67},{4,68},{5,69},{6,70},{7,71},{8,72},{9,... | collective-permute-start | bytes 3145736 | tf_op jit(solution)/shard_map/while/body/eval_jaxpr/ppermute | solution.py:32
  219.9 37.6 %all-gather.12.cloned.1.call-start = ((), (), s32[]{:S(2)}) async-start(), calls=%async_computation.5 | async-start | bytes 2621440 | tf_op jit(solution)/shard_map/while/body/eval_jaxpr/all_gather | solution.py:26
  265.1 25.6 %collective-permute-start = (bf16[128,4096]{1,0:T(8,128)(2,1)}, bf16[128,4096]{1,0:T(8,128)(2,1)S(1)}, u32[]{:S(2)}, u32[]{:S(2)}) collective-permute-start(bf16[128,4096]{1,0:T(8,128)(2,1)} %get-tuple-element.782), channel_id=1, source_target_pairs={{0,64},{1,65},{2,66},{3,67},{4,68},{5,69},{6,70},{7,71},{8,72},{9,... | collective-permute-start | bytes 3145736 | tf_op jit(solution)/shard_map/while/body/eval_jaxpr/ppermute | solution.py:32
  291.7 38.2 %all-gather.12.cloned.1.call-start = ((), (), s32[]{:S(2)}) async-start(), calls=%async_computation.5 | async-start | bytes 2621440 | tf_op jit(solution)/shard_map/while/body/eval_jaxpr/all_gather | solution.py:26
  332.9 30.1 %collective-permute-start = (bf16[128,4096]{1,0:T(8,128)(2,1)}, bf16[128,4096]{1,0:T(8,128)(2,1)S(1)}, u32[]{:S(2)}, u32[]{:S(2)}) collective-permute-start(bf16[128,4096]{1,0:T(8,128)(2,1)} %get-tuple-element.782), channel_id=1, source_target_pairs={{0,64},{1,65},{2,66},{3,67},{4,68},{5,69},{6,70},{7,71},{8,72},{9,... | collective-permute-start | bytes 3145736 | tf_op jit(solution)/shard_map/while/body/eval_jaxpr/ppermute | solution.py:32
  364.0 8.8 copy-start.4
  381.8 37.8 %all-gather.14.cloned.1.call-start = ((), (), s32[]{:S(2)}) async-start(), calls=%async_computation.6 | async-start | bytes 2621440 | tf_op jit(solution)/shard_map/while/body/eval_jaxpr/all_gather | solution.py:26
  384.5 37.0 %copy-start.5 = (f32[2,128,1024]{2,1,0:T(8,128)S(1)}, f32[2,128,1024]{2,1,0:T(8,128)}, u32[]{:S(2)}) copy-start(f32[2,128,1024]{2,1,0:T(8,128)} %get-tuple-element.773) | copy-start | bytes 3145732 | tf_op jit(solution)/shard_map/while
  422.8 31.7 %collective-permute-start.1 = (bf16[128,4096]{1,0:T(8,128)(2,1)}, bf16[128,4096]{1,0:T(8,128)(2,1)S(1)}, u32[]{:S(2)}, u32[]{:S(2)}) collective-permute-start(bf16[128,4096]{1,0:T(8,128)(2,1)} %copy-done.7), channel_id=1, source_target_pairs={{64,0},{65,1},{66,2},{67,3},{68,4},{69,5},{70,6},{71,7},{72,8},{73... | collective-permute-start | bytes 3145736 | tf_op jit(solution)/shard_map/while/body/eval_jaxpr/ppermute | solution.py:32
  454.6 37.3 %all-gather.14.cloned.1.call-start = ((), (), s32[]{:S(2)}) async-start(), calls=%async_computation.6 | async-start | bytes 2621440 | tf_op jit(solution)/shard_map/while/body/eval_jaxpr/all_gather | solution.py:26
  457.1 36.5 %copy-start.5 = (f32[2,128,1024]{2,1,0:T(8,128)S(1)}, f32[2,128,1024]{2,1,0:T(8,128)}, u32[]{:S(2)}) copy-start(f32[2,128,1024]{2,1,0:T(8,128)} %get-tuple-element.773) | copy-start | bytes 3145732 | tf_op jit(solution)/shard_map/while
  500.2 1.0 copy-start.7
  501.2 27.4 %collective-permute-start.1 = (bf16[128,4096]{1,0:T(8,128)(2,1)}, bf16[128,4096]{1,0:T(8,128)(2,1)S(1)}, u32[]{:S(2)}, u32[]{:S(2)}) collective-permute-start(bf16[128,4096]{1,0:T(8,128)(2,1)} %copy-done.7), channel_id=1, source_target_pairs={{64,0},{65,1},{66,2},{67,3},{68,4},{69,5},{70,6},{71,7},{72,8},{73... | collective-permute-start | bytes 3145736 | tf_op jit(solution)/shard_map/while/body/eval_jaxpr/ppermute | solution.py:32
  502.5 12.9 %copy-start = (bf16[1,1024,4096]{2,1,0:T(8,128)(2,1)S(1)}, bf16[1,1024,4096]{2,1,0:T(8,128)(2,1)}, u32[]{:S(2)}) copy-start(bf16[1,1024,4096]{2,1,0:T(8,128)(2,1)} %get-tuple-element.374) | copy-start | bytes 25165828 | tf_op jit(solution)/shard_map/while/body/eval_jaxpr/cond
  524.7 3.4 copy-start.1
  528.5 35.4 %all-gather.14.cloned.1.call-start = ((), (), s32[]{:S(2)}) async-start(), calls=%async_computation.6 | async-start | bytes 2621440 | tf_op jit(solution)/shard_map/while/body/eval_jaxpr/all_gather | solution.py:26
  531.1 34.6 %copy-start.5 = (f32[2,128,1024]{2,1,0:T(8,128)S(1)}, f32[2,128,1024]{2,1,0:T(8,128)}, u32[]{:S(2)}) copy-start(f32[2,128,1024]{2,1,0:T(8,128)} %get-tuple-element.773) | copy-start | bytes 3145732 | tf_op jit(solution)/shard_map/while
  573.2 27.4 %collective-permute-start.1 = (bf16[128,4096]{1,0:T(8,128)(2,1)}, bf16[128,4096]{1,0:T(8,128)(2,1)S(1)}, u32[]{:S(2)}, u32[]{:S(2)}) collective-permute-start(bf16[128,4096]{1,0:T(8,128)(2,1)} %copy-done.7), channel_id=1, source_target_pairs={{64,0},{65,1},{66,2},{67,3},{68,4},{69,5},{70,6},{71,7},{72,8},{73... | collective-permute-start | bytes 3145736 | tf_op jit(solution)/shard_map/while/body/eval_jaxpr/ppermute | solution.py:32
  574.5 12.9 %copy-start = (bf16[1,1024,4096]{2,1,0:T(8,128)(2,1)S(1)}, bf16[1,1024,4096]{2,1,0:T(8,128)(2,1)}, u32[]{:S(2)}) copy-start(bf16[1,1024,4096]{2,1,0:T(8,128)(2,1)} %get-tuple-element.374) | copy-start | bytes 25165828 | tf_op jit(solution)/shard_map/while/body/eval_jaxpr/cond
  596.7 3.4 copy-start.1
  600.6 122.3 %reduce-scatter.5.cloned.1.call-start = ((), (), s32[]{:S(2)}) async-start(), calls=%async_computation.4 | async-start | bytes 17825792 | tf_op jit(solution)/shard_map/reduce_scatter | solution.py:190
  612.8 223.7 %reduce-scatter.3.cloned.1.call-start = ((), (), s32[]{:S(2)}) async-start(), calls=%async_computation.3 | async-start | bytes 17825792 | tf_op jit(solution)/shard_map/reduce_scatter | solution.py:189
  (11 other events, 9.6 us)
Sparse Core Ops, SparseCore 0:
  10.7 113.8 all-gather.9
  160.5 26.1 all-gather.11
  229.9 27.5 all-gather.11
  297.1 32.7 all-gather.11
  385.5 34.1 all-gather.13
  464.5 27.3 all-gather.13
  538.4 25.4 all-gather.13
  612.9 109.9 reduce-scatter.4
  726.3 110.0 reduce-scatter.2
where the time goes:
time: 890 us; the launch traced here: 888 us
  waiting for transfers between devices  597 us (67%)
  matrix products  90.1 us (10%)
  local copies, waits for them, and re-layouts  66.9 us (8%)
  other arithmetic  62.4 us (7%)
  blocking collectives  35.5 us (4%)
  between operations  17 us (2%)
  starting transfers between devices  15 us (2%)
    all_gather x6, waiting for transfers between devices, total_of_pieces(): return lax.all_gather(value, axis).sum(0)  174 us
    all_gather x1, waiting for transfers between devices, rows_first(): filled, at, done = (lax.all_gather(both, axis, axis=0, tiled=True), 0, [])  114 us
    reduce_scatter x1, waiting for transfers between devices, on_device(): lax.psum_scatter(total_in, DP, scatter_dimension=0, tiled=True)  111 us
    ppermute x6, waiting for transfers between devices, from_behind(): return lax.ppermute(value, axis, pairs)  100 us
    reduce_scatter x1, waiting for transfers between devices, on_device(): lax.psum_scatter(total_out, DP, scatter_dimension=1, tiled=True)  96.8 us
    psum x5, blocking collectives, by_axis(): value = lax.psum(value, axis)  35.5 us
    dot_general x2, matrix products, accumulate(): jnp.einsum('gtc,gth->gch', x_groups, slope_groups, preferred_element_type...  25.8 us
    dot_general x4, matrix products, contract_last(): lax.dot_general(first_operand, second_operand, (((1,), (1,)), ((), ())),...  25.2 us
  transfers between devices with their start and end apart: 15, of which 15 were waited for; matrix products, arithmetic and copies ran while one was open for 7% of the time, Pallas kernels for 0%

commit v1 on v0

--- a/solution.py
+++ b/solution.py
@@ -14,7 +14,13 @@
 def rows_first(arrays, axis, dims):
     turned = [jnp.moveaxis(a, dim, 0) for a, dim in zip(arrays, dims)]
     both = jnp.concatenate([t.reshape(len(t), -1) for t in turned], axis=1)
-    filled, at, done = (lax.all_gather(both, axis, axis=0, tiled=True), 0, [])
+    filled, at, done = (
+        jnp.concatenate(
+            lax.all_to_all(jnp.stack([both] * lax.axis_size(axis)), axis, 0, 0), axis=0
+        ),
+        0,
+        [],
+    )
     for t, dim in zip(turned, dims):
         section = filled[:, at : at + t[0].size].reshape(-1, *t.shape[1:])
         done.append(jnp.moveaxis(section, 0, dim))

time: 890 us -> 1040 us (1.17)
  waiting for transfers between devices: 597 us -> 730 us
    all_to_all x0 -> x1, waiting for transfers between devices: none -> 250 us  [rows_first(): lax.all_to_all(jnp.stack([both] * lax.axis_size(axis)), axis, 0, 0)]
    all_gather x1 -> x0, waiting for transfers between devices: 114 us -> none  [rows_first(): filled, at, done = (lax.all_gather(both, axis, axis=0, tiled=True), 0, [])]
    another operation x4 -> x5, local copies, waits for them, and re-layouts: 17.5 us -> 23.5 us
  transfers between devices with their start and end apart: 15 -> 15, of which waited for: 15 -> 15; matrix products, arithmetic and copies ran while one was open for 7% -> 6% of each run, Pallas kernels for 0% -> 0%
where the time goes in v1:
time: 1040 us
  waiting for transfers between devices  730 us (70%)
  matrix products  90.1 us (9%)
  local copies, waits for them, and re-layouts  73.7 us (7%)
  other arithmetic  61.5 us (6%)
  blocking collectives  35.5 us (3%)
  starting transfers between devices  23.1 us (2%)
  between operations  18.7 us (2%)
    all_to_all x1, waiting for transfers between devices, rows_first(): lax.all_to_all(jnp.stack([both] * lax.axis_size(axis)), axis, 0, 0)  250 us
    all_gather x6, waiting for transfers between devices, total_of_pieces(): return lax.all_gather(value, axis).sum(0)  172 us
    reduce_scatter x1, waiting for transfers between devices, on_device(): lax.psum_scatter(total_in, DP, scatter_dimension=0, tiled=True)  111 us
    ppermute x6, waiting for transfers between devices, from_behind(): return lax.ppermute(value, axis, pairs)  100 us
    reduce_scatter x1, waiting for transfers between devices, on_device(): lax.psum_scatter(total_out, DP, scatter_dimension=1, tiled=True)  96.6 us
    psum x5, blocking collectives, by_axis(): value = lax.psum(value, axis)  35.5 us
    dot_general x2, matrix products, accumulate(): jnp.einsum('gtc,gth->gch', x_groups, slope_groups, preferred_element_type...  25.8 us
    dot_general x4, matrix products, contract_last(): lax.dot_general(first_operand, second_operand, (((1,), (1,)), ((), ())),...  25.2 us
  transfers between devices with their start and end apart: 15, of which 15 were waited for; matrix products, arithmetic and copies ran while one was open for 6% of the time, Pallas kernels for 0%

profile of v1, /device:TPU:0, one launch (start us, length us, event | category | flops | bytes accessed | tf_op | source)
XLA Modules:
  0.0 1037.9 jit_solution(12473234596837517246)
XLA Ops:
  25.2 249.9 %all-to-all-done = bf16[16,256,2048]{2,1,0:T(8,128)(2,1)} async-done(((bf16[16,256,2048]{2,1,0:T(8,128)(2,1)}), bf16[16,256,2048]{2,1,0:T(8,128)(2,1)}, u32[]{:S(2)}, u32[]{:S(2)}) %all-to-all-start) | async-done | bytes 16777248 | tf_op jit(solution)/shard_map/all_to_all | solution.py:19
  275.2 11.7 %fusion.32 = (bf16[4096,1024]{1,0:T(8,128)(2,1)}, bf16[1024,4096]{0,1:T(8,128)(2,1)}) fusion(bf16[4096,2048]{1,0:T(8,128)(2,1)} %bitcast.16), kind=kLoop, calls=%fused_computation.55 | loop fusion | bytes 33554432 | tf_op jit(solution)/shard_map/slice | solution.py:25
  286.8 11.6 %copy.10 = bf16[1024,4096]{1,0:T(8,128)(2,1)} copy(bf16[1024,4096]{0,1:T(8,128)(2,1)} %get-tuple-element.500) | data formatting | bytes 16777216 | tf_op jit(solution)/shard_map/while | solution.py:187
  301.2 211.9 %while.37 = (s32[]{:T(128)}, bf16[128,4096]{1,0:T(8,128)(2,1)}, bf16[2,128,4096]{2,1,0:T(8,128)(2,1)}, f32[2,128,1024]{2,1,0:T(8,128)S(1)}, bf16[2,128,1024]{2,1...) while((s32[]{:T(128)}, bf16[128,4096]{1,0:T(8,128)(2,1)}, ...), condition=%wide.region_6.7_spmd, body=%wide.region_0.6_spmd.sunk | while | flops 2152071168 | bytes 50332584 | solution.py:145
  311.2 24.4 %all-gather.9.cloned.1.call-done = f32[512,1024]{1,0:T(8,128)} async-done(((f32[128,1024]{1,0:T(8,128)}), f32[512,1024]{1,0:T(8,128)}) %all-gather.9.cloned.1.call-update) | async-done | bytes 2097168 | tf_op jit(solution)/shard_map/while/body/eval_jaxpr/all_gather | solution.py:32
  344.9 23.0 %collective-permute-done = bf16[128,4096]{1,0:T(8,128)(2,1)S(1)} collective-permute-done((bf16[128,4096]{1,0:T(8,128)(2,1)}, bf16[128,4096]{1,0:T(8,128)(2,1)S(1)}, u32[]{:S(2)}, u32[]{:S(2)}) %collective-permute-start) | collective-permute-done | bytes 1048608 | tf_op jit(solution)/shard_map/while/body/eval_jaxpr/ppermute | solution.py:38
  378.8 27.7 %all-gather.9.cloned.1.call-done = f32[512,1024]{1,0:T(8,128)} async-done(((f32[128,1024]{1,0:T(8,128)}), f32[512,1024]{1,0:T(8,128)}) %all-gather.9.cloned.1.call-update) | async-done | bytes 2097168 | tf_op jit(solution)/shard_map/while/body/eval_jaxpr/all_gather | solution.py:32
  416.9 22.8 %collective-permute-done = bf16[128,4096]{1,0:T(8,128)(2,1)S(1)} collective-permute-done((bf16[128,4096]{1,0:T(8,128)(2,1)}, bf16[128,4096]{1,0:T(8,128)(2,1)S(1)}, u32[]{:S(2)}, u32[]{:S(2)}) %collective-permute-start) | collective-permute-done | bytes 1048608 | tf_op jit(solution)/shard_map/while/body/eval_jaxpr/ppermute | solution.py:38
  446.1 32.9 %all-gather.9.cloned.1.call-done = f32[512,1024]{1,0:T(8,128)} async-done(((f32[128,1024]{1,0:T(8,128)}), f32[512,1024]{1,0:T(8,128)}) %all-gather.9.cloned.1.call-update) | async-done | bytes 2097168 | tf_op jit(solution)/shard_map/while/body/eval_jaxpr/all_gather | solution.py:32
  489.4 22.8 %collective-permute-done = bf16[128,4096]{1,0:T(8,128)(2,1)S(1)} collective-permute-done((bf16[128,4096]{1,0:T(8,128)(2,1)}, bf16[128,4096]{1,0:T(8,128)(2,1)S(1)}, u32[]{:S(2)}, u32[]{:S(2)}) %collective-permute-start) | collective-permute-done | bytes 1048608 | tf_op jit(solution)/shard_map/while/body/eval_jaxpr/ppermute | solution.py:38
  530.7 218.9 %while.38 = (s32[]{:T(128)}, bf16[128,4096]{1,0:T(8,128)(2,1)S(1)}, bf16[1,4096,1024]{2,1,0:T(8,128)(2,1)}, bf16[1,4096,1024]{2,1,0:T(8,128)(2,1)}, bf16[1,1024,...) while((s32[]{:T(128)}, bf16[128,4096]{1,0:T(8,128)(2,1)S(1)}, ...), condition=%wide.region_15.16_spmd, body=%wide.region_7.15_spmd.sunk | while | flops 4374134784 | bytes 187172016 | solution.py:187
  534.5 34.3 %all-gather.11.cloned.1.call-done = f32[512,1024]{1,0:T(8,128)} async-done(((f32[128,1024]{1,0:T(8,128)}), f32[512,1024]{1,0:T(8,128)}) %all-gather.11.cloned.1.call-update) | async-done | bytes 2097168 | tf_op jit(solution)/shard_map/while/body/eval_jaxpr/all_gather | solution.py:32
  573.2 30.4 %collective-permute-done.1 = bf16[128,4096]{1,0:T(8,128)(2,1)S(1)} collective-permute-done((bf16[128,4096]{1,0:T(8,128)(2,1)}, bf16[128,4096]{1,0:T(8,128)(2,1)S(1)}, u32[]{:S(2)}, u32[]{:S(2)}) %collective-permute-start.1) | collective-permute-done | bytes 1048608 | tf_op jit(solution)/shard_map/while/body/eval_jaxpr/ppermute | solution.py:38
  613.4 27.5 %all-gather.11.cloned.1.call-done = f32[512,1024]{1,0:T(8,128)} async-done(((f32[128,1024]{1,0:T(8,128)}), f32[512,1024]{1,0:T(8,128)}) %all-gather.11.cloned.1.call-update) | async-done | bytes 2097168 | tf_op jit(solution)/shard_map/while/body/eval_jaxpr/all_gather | solution.py:32
  651.5 25.6 %conditional.14 = ((bf16[1,4096,1024]{2,1,0:T(8,128)(2,1)}, bf16[1,4096,1024]{2,1,0:T(8,128)(2,1)}, bf16[1,1024,4096]{2,1,0:T(8,128)(2,1)}, bf16[1,1024,4096]{2,1,0:T(8,128)(2,1)})) conditional(s32[]{:T(128)} %convert_element_type.173, (bf16[1,4096,1024]{2,1,0:T(8,128)(2,1)}, bf16[1,4096,1024]{2,1,0:T(8,128)(2,1)}, ...), branch_computations={%region_13.13_spmd, %region_14.14_spmd} | conditional | flops 2222981120 | bytes 136839776 | solution.py:176
  651.5 12.9 %fusion.12 = (bf16[1,4096,1024]{2,1,0:T(8,128)(2,1)}, bf16[1,4096,1024]{2,1,0:T(8,128)(2,1)}) fusion(bf16[1,4096,1024]{2,1,0:T(8,128)(2,1)} %get-tuple-element.369, bf16[1,4096,1024]{2,1,0:T(8,128)(2,1)} %get-tuple-element.373, bf16[128,1024]{1,0:T(8,128)(2,1)S(1)} %get-tuple-element.372, bf16[2,128,4096]{2,1,0:T(8,128)(2,1)} %get-tuple-element.370, ...), kind=kOutput, calls=%fused_computation.24 | convolution fusion | flops 1111490560 | bytes 34865664 | tf_op jit(solution)/shard_map/while/body/eval_jaxpr/cond/branch_1_fun/gtc,gth->gch/dot_general | solution.py:154
  687.4 25.6 %all-gather.11.cloned.1.call-done = f32[512,1024]{1,0:T(8,128)} async-done(((f32[128,1024]{1,0:T(8,128)}), f32[512,1024]{1,0:T(8,128)}) %all-gather.11.cloned.1.call-update) | async-done | bytes 2097168 | tf_op jit(solution)/shard_map/while/body/eval_jaxpr/all_gather | solution.py:32
  723.6 25.6 %conditional.14 = ((bf16[1,4096,1024]{2,1,0:T(8,128)(2,1)}, bf16[1,4096,1024]{2,1,0:T(8,128)(2,1)}, bf16[1,1024,4096]{2,1,0:T(8,128)(2,1)}, bf16[1,1024,4096]{2,1,0:T(8,128)(2,1)})) conditional(s32[]{:T(128)} %convert_element_type.173, (bf16[1,4096,1024]{2,1,0:T(8,128)(2,1)}, bf16[1,4096,1024]{2,1,0:T(8,128)(2,1)}, ...), branch_computations={%region_13.13_spmd, %region_14.14_spmd} | conditional | flops 2222981120 | bytes 136839776 | solution.py:176
  723.6 12.9 %fusion.12 = (bf16[1,4096,1024]{2,1,0:T(8,128)(2,1)}, bf16[1,4096,1024]{2,1,0:T(8,128)(2,1)}) fusion(bf16[1,4096,1024]{2,1,0:T(8,128)(2,1)} %get-tuple-element.369, bf16[1,4096,1024]{2,1,0:T(8,128)(2,1)} %get-tuple-element.373, bf16[128,1024]{1,0:T(8,128)(2,1)S(1)} %get-tuple-element.372, bf16[2,128,4096]{2,1,0:T(8,128)(2,1)} %get-tuple-element.370, ...), kind=kOutput, calls=%fused_computation.24 | convolution fusion | flops 1111490560 | bytes 34865664 | tf_op jit(solution)/shard_map/while/body/eval_jaxpr/cond/branch_1_fun/gtc,gth->gch/dot_general | solution.py:154
  749.6 12.2 %subtract_bitcast_fusion = f32[1024,4096]{1,0:T(8,128)} fusion(bf16[1,1024,4096]{2,1,0:T(8,128)(2,1)} %get-tuple-element.414, bf16[1,1024,4096]{2,1,0:T(8,128)(2,1)} %get-tuple-element.413), kind=kLoop, calls=%fused_computation.47 | loop fusion | flops 12582912 | bytes 33554432 | tf_op jit(solution)/shard_map/reduce_sum | solution.py:193
  761.9 13.3 %subtract_bitcast_fusion.1 = f32[4096,1024]{1,0:T(8,128)} fusion(bf16[1,4096,1024]{2,1,0:T(8,128)(2,1)} %get-tuple-element.412, bf16[1,4096,1024]{2,1,0:T(8,128)(2,1)} %get-tuple-element.411), kind=kLoop, calls=%fused_computation.48 | loop fusion | flops 12582912 | bytes 33554432 | tf_op jit(solution)/shard_map/reduce_sum | solution.py:192
  775.2 96.6 %reduce-scatter.5.cloned.1.call-done = f32[1024,256]{1,0:T(8,128)} async-done(((f32[1024,4096]{1,0:T(8,128)}), f32[1024,256]{1,0:T(8,128)}) %reduce-scatter.5.cloned.1.call-update) | async-done | bytes 1048592 | tf_op jit(solution)/shard_map/reduce_scatter | solution.py:196
  873.9 111.2 %reduce-scatter.3.cloned.1.call-done = f32[256,1024]{1,0:T(8,128)} async-done(((f32[4096,1024]{1,0:T(8,128)}), f32[256,1024]{1,0:T(8,128)}) %reduce-scatter.3.cloned.1.call-update) | async-done | bytes 1048592 | tf_op jit(solution)/shard_map/reduce_scatter | solution.py:195
  1004.1 10.6 %psum.38 = f32[]{:T(128)} all-reduce(f32[]{:T(128)} %psum.37), channel_id=1, replica_groups=mesh['pipe'=2,'tensor_0'=2,'tensor_1'=2,'dp_0'=4,'dp_1'=4] {'dp_0'}, use_global_device_ids=true, to_apply=%region_23.24 | all-reduce | flops 1 | bytes 8 | tf_op jit(solution)/shard_map/psum | solution.py:43
  (145 shorter events, 247.2 us)
Async XLA Ops:
  17.0 258.2 %all-to-all-start = ((bf16[16,256,2048]{2,1,0:T(8,128)(2,1)}), bf16[16,256,2048]{2,1,0:T(8,128)(2,1)}, u32[]{:S(2)}, u32[]{:S(2)}) async-start(bf16[16,256,2048]{2,1,0:T(8,128)(2,1)} %stack.2), calls=%async_computation | async-start | bytes 33554432 | tf_op jit(solution)/shard_map/all_to_all | solution.py:19
  301.2 34.4 %all-gather.9.cloned.1.call-start = ((), (), s32[]{:S(2)}) async-start(), calls=%async_computation.5 | async-start | bytes 2621440 | tf_op jit(solution)/shard_map/while/body/eval_jaxpr/all_gather | solution.py:32
  343.2 24.7 %collective-permute-start = (bf16[128,4096]{1,0:T(8,128)(2,1)}, bf16[128,4096]{1,0:T(8,128)(2,1)S(1)}, u32[]{:S(2)}, u32[]{:S(2)}) collective-permute-start(bf16[128,4096]{1,0:T(8,128)(2,1)} %get-tuple-element.782), channel_id=1, source_target_pairs={{0,64},{1,65},{2,66},{3,67},{4,68},{5,69},{6,70},{7,71},{8,72},{9,... | collective-permute-start | bytes 3145736 | tf_op jit(solution)/shard_map/while/body/eval_jaxpr/ppermute | solution.py:38
  368.9 37.6 %all-gather.9.cloned.1.call-start = ((), (), s32[]{:S(2)}) async-start(), calls=%async_computation.5 | async-start | bytes 2621440 | tf_op jit(solution)/shard_map/while/body/eval_jaxpr/all_gather | solution.py:32
  414.1 25.6 %collective-permute-start = (bf16[128,4096]{1,0:T(8,128)(2,1)}, bf16[128,4096]{1,0:T(8,128)(2,1)S(1)}, u32[]{:S(2)}, u32[]{:S(2)}) collective-permute-start(bf16[128,4096]{1,0:T(8,128)(2,1)} %get-tuple-element.782), channel_id=1, source_target_pairs={{0,64},{1,65},{2,66},{3,67},{4,68},{5,69},{6,70},{7,71},{8,72},{9,... | collective-permute-start | bytes 3145736 | tf_op jit(solution)/shard_map/while/body/eval_jaxpr/ppermute | solution.py:38
  440.7 38.3 %all-gather.9.cloned.1.call-start = ((), (), s32[]{:S(2)}) async-start(), calls=%async_computation.5 | async-start | bytes 2621440 | tf_op jit(solution)/shard_map/while/body/eval_jaxpr/all_gather | solution.py:32
  482.0 30.1 %collective-permute-start = (bf16[128,4096]{1,0:T(8,128)(2,1)}, bf16[128,4096]{1,0:T(8,128)(2,1)S(1)}, u32[]{:S(2)}, u32[]{:S(2)}) collective-permute-start(bf16[128,4096]{1,0:T(8,128)(2,1)} %get-tuple-element.782), channel_id=1, source_target_pairs={{0,64},{1,65},{2,66},{3,67},{4,68},{5,69},{6,70},{7,71},{8,72},{9,... | collective-permute-start | bytes 3145736 | tf_op jit(solution)/shard_map/while/body/eval_jaxpr/ppermute | solution.py:38
  513.1 8.8 copy-start.4
  530.9 37.8 %all-gather.11.cloned.1.call-start = ((), (), s32[]{:S(2)}) async-start(), calls=%async_computation.6 | async-start | bytes 2621440 | tf_op jit(solution)/shard_map/while/body/eval_jaxpr/all_gather | solution.py:32
  533.6 37.0 %copy-start.5 = (f32[2,128,1024]{2,1,0:T(8,128)S(1)}, f32[2,128,1024]{2,1,0:T(8,128)}, u32[]{:S(2)}) copy-start(f32[2,128,1024]{2,1,0:T(8,128)} %get-tuple-element.773) | copy-start | bytes 3145732 | tf_op jit(solution)/shard_map/while
  570.9 1.0 copy-start.7
  571.9 31.7 %collective-permute-start.1 = (bf16[128,4096]{1,0:T(8,128)(2,1)}, bf16[128,4096]{1,0:T(8,128)(2,1)S(1)}, u32[]{:S(2)}, u32[]{:S(2)}) collective-permute-start(bf16[128,4096]{1,0:T(8,128)(2,1)} %copy-done.7), channel_id=1, source_target_pairs={{64,0},{65,1},{66,2},{67,3},{68,4},{69,5},{70,6},{71,7},{72,8},{73... | collective-permute-start | bytes 3145736 | tf_op jit(solution)/shard_map/while/body/eval_jaxpr/ppermute | solution.py:38
  603.6 37.3 %all-gather.11.cloned.1.call-start = ((), (), s32[]{:S(2)}) async-start(), calls=%async_computation.6 | async-start | bytes 2621440 | tf_op jit(solution)/shard_map/while/body/eval_jaxpr/all_gather | solution.py:32
  606.2 36.5 %copy-start.5 = (f32[2,128,1024]{2,1,0:T(8,128)S(1)}, f32[2,128,1024]{2,1,0:T(8,128)}, u32[]{:S(2)}) copy-start(f32[2,128,1024]{2,1,0:T(8,128)} %get-tuple-element.773) | copy-start | bytes 3145732 | tf_op jit(solution)/shard_map/while
  650.2 27.4 %collective-permute-start.1 = (bf16[128,4096]{1,0:T(8,128)(2,1)}, bf16[128,4096]{1,0:T(8,128)(2,1)S(1)}, u32[]{:S(2)}, u32[]{:S(2)}) collective-permute-start(bf16[128,4096]{1,0:T(8,128)(2,1)} %copy-done.7), channel_id=1, source_target_pairs={{64,0},{65,1},{66,2},{67,3},{68,4},{69,5},{70,6},{71,7},{72,8},{73... | collective-permute-start | bytes 3145736 | tf_op jit(solution)/shard_map/while/body/eval_jaxpr/ppermute | solution.py:38
  651.5 12.9 %copy-start = (bf16[1,1024,4096]{2,1,0:T(8,128)(2,1)S(1)}, bf16[1,1024,4096]{2,1,0:T(8,128)(2,1)}, u32[]{:S(2)}) copy-start(bf16[1,1024,4096]{2,1,0:T(8,128)(2,1)} %get-tuple-element.374) | copy-start | bytes 25165828 | tf_op jit(solution)/shard_map/while/body/eval_jaxpr/cond
  673.7 3.3 copy-start.1
  677.6 35.4 %all-gather.11.cloned.1.call-start = ((), (), s32[]{:S(2)}) async-start(), calls=%async_computation.6 | async-start | bytes 2621440 | tf_op jit(solution)/shard_map/while/body/eval_jaxpr/all_gather | solution.py:32
  680.2 34.6 %copy-start.5 = (f32[2,128,1024]{2,1,0:T(8,128)S(1)}, f32[2,128,1024]{2,1,0:T(8,128)}, u32[]{:S(2)}) copy-start(f32[2,128,1024]{2,1,0:T(8,128)} %get-tuple-element.773) | copy-start | bytes 3145732 | tf_op jit(solution)/shard_map/while
  722.3 27.4 %collective-permute-start.1 = (bf16[128,4096]{1,0:T(8,128)(2,1)}, bf16[128,4096]{1,0:T(8,128)(2,1)S(1)}, u32[]{:S(2)}, u32[]{:S(2)}) collective-permute-start(bf16[128,4096]{1,0:T(8,128)(2,1)} %copy-done.7), channel_id=1, source_target_pairs={{64,0},{65,1},{66,2},{67,3},{68,4},{69,5},{70,6},{71,7},{72,8},{73... | collective-permute-start | bytes 3145736 | tf_op jit(solution)/shard_map/while/body/eval_jaxpr/ppermute | solution.py:38
  723.6 12.9 %copy-start = (bf16[1,1024,4096]{2,1,0:T(8,128)(2,1)S(1)}, bf16[1,1024,4096]{2,1,0:T(8,128)(2,1)}, u32[]{:S(2)}) copy-start(bf16[1,1024,4096]{2,1,0:T(8,128)(2,1)} %get-tuple-element.374) | copy-start | bytes 25165828 | tf_op jit(solution)/shard_map/while/body/eval_jaxpr/cond
  745.8 3.3 copy-start.1
  749.6 122.1 %reduce-scatter.5.cloned.1.call-start = ((), (), s32[]{:S(2)}) async-start(), calls=%async_computation.4 | async-start | bytes 17825792 | tf_op jit(solution)/shard_map/reduce_scatter | solution.py:196
  761.8 223.3 %reduce-scatter.3.cloned.1.call-start = ((), (), s32[]{:S(2)}) async-start(), calls=%async_computation.3 | async-start | bytes 17825792 | tf_op jit(solution)/shard_map/reduce_scatter | solution.py:195
  (11 other events, 9.6 us)
Sparse Core Ops, SparseCore 0:
  311.3 24.2 all-gather.8
  379.0 27.5 all-gather.8
  446.2 32.7 all-gather.8
  534.6 34.1 all-gather.10
  613.5 27.3 all-gather.10
  687.5 25.4 all-gather.10
Sparse Core Ops, SparseCore 1:
  761.9 109.8 reduce-scatter.4
  875.1 110.0 reduce-scatter.2
